TPU v7x, 256 devices: a whole 4x4x8 slice. The times are simulated.
256 devices in a mesh: tp: 4 (over x), dp: 64 (over z, y, core).
Axes of the slice: x: 4, y: 4, z: 8, core: 2. Of those that a mesh axis runs over, the one named last changes fastest.
Arguments:
- item_query: bfloat16 [8192, 2048], P('dp', 'tp'), may hold values from -20 to 20, as said below
- item_keys: bfloat16 [8192, 4, 2048], P('dp', None, 'tp'), may hold values from -20 to 20
- item_values: bfloat16 [8192, 4, 2048], P('dp', None, 'tp'), may hold values from -6 to 6
- item_out_weight: bfloat16 [2048, 4096], P('tp'), may hold values from -0.125 to 0.125
- item_residual: bfloat16 [8192, 4096], P('dp'), may hold values from -3 to 3
- cite_home: int32 [65536, 1], P('dp'), may hold values from 0 to 63; in each aligned block of 1024 rows (0 to 1023, 1024 to 2047, ...) at most 24 rows name the same one
- cite_row: int32 [65536], P('dp'), may hold values from 0 to 127
- seq_length: int32 [64], P('dp'), may hold values from 1 to 1024, 40960 in all
- user_gain: float32 [4096], replicated, may hold values from 0.1 to 1.9
- user_weight: bfloat16 [4096, 16, 384], P('dp', 'tp'), may hold values from -0.09375 to 0.09375
Outputs:
- user_qkv: bfloat16 [65536, 16, 384], P('dp', 'tp')
Inputs may be any that keep to these rules, and one draw needn't show every extreme that they name: `item_query`: in hidden draws some items' queries equal a multiple of keys at their last two tokens. `cite_home`: among the 1024 positions of one sequence at most 24 cite items of one home device, and some home device is cited exactly 24 times. `seq_length`: some sequence has all 1024 positions live.
All inputs are finite; a program needn't handle non-finite values. No bound on the sum of `seq_length` on one device may be relied on, other than what follows from the above.
Results may differ from a plain program's by a relative error of at most 0.0065.
Values may be sent and summed in bfloat16 or wider, within the bound.
No kernel may reach another device: no remote copies, remote signals or barrier semaphores. Data moves between devices by JAX's collectives and lax.ppermute only.
A program may use at most 128 MiB of HBM per device.

v0:
```python
import math
import jax
import jax.numpy as jnp
from jax import lax
from jax.sharding import PartitionSpec as P

HEAD_DIM = 128


def cut_along(x, dim, size):
    before, after = (x.shape[:dim], x.shape[dim + 1 :])
    return jnp.moveaxis(x.reshape(*before, size, -1, *after), dim, 0)


def sent_and_summed(x, axis, dim):
    parts = cut_along(x, dim, lax.axis_size(axis))
    arrived = lax.all_to_all(parts, axis, split_axis=0, concat_axis=0, tiled=True)
    return arrived.sum(axis=0)


def per_device(
    item_query,
    item_keys,
    item_values,
    item_out_weight,
    item_residual,
    cite_home,
    cite_row,
    seq_length,
    user_gain,
    user_weight,
):
    count_items, width_heads = item_query.shape
    tokens_item = item_keys.shape[1]
    local_heads = width_heads // HEAD_DIM
    queries = item_query.reshape(count_items, local_heads, HEAD_DIM)
    keys_all = item_keys.reshape(count_items, tokens_item, local_heads, HEAD_DIM)
    values_all = item_values.reshape(count_items, tokens_item, local_heads, HEAD_DIM)
    scores = jnp.einsum("ihd,ithd->iht", queries, keys_all, preferred_element_type=jnp.float32) * (
        1.0 / math.sqrt(HEAD_DIM)
    )
    probs = jax.nn.softmax(scores, axis=-1).astype(jnp.bfloat16)
    attended = jnp.einsum("iht,ithd->ihd", probs, values_all, preferred_element_type=jnp.float32)
    attended = attended.astype(jnp.bfloat16).reshape(count_items, width_heads)
    partial_value = jnp.dot(attended, item_out_weight, preferred_element_type=jnp.float32)
    summed = sent_and_summed(partial_value, "tp", 1)
    columns = summed.shape[1]
    own_cols = lax.dynamic_slice_in_dim(item_residual, lax.axis_index("tp") * columns, columns, 1)
    item_vec = (summed + own_cols.astype(jnp.float32)).astype(jnp.bfloat16)
    home_dev = cite_home[:, 0]
    length_seq = home_dev.shape[0]
    devices = lax.axis_size("dp")
    capacity = 3 * length_seq // (2 * devices)
    onehot = (home_dev[:, None] == jnp.arange(devices, dtype=jnp.int32)[None, :]).astype(jnp.int32)
    before = jnp.cumsum(onehot, axis=0) - onehot
    slot_index = jnp.sum(before * onehot, axis=1)
    target = home_dev * capacity + slot_index
    wanted = (
        jnp.zeros((devices * capacity,), jnp.int32)
        .at[target]
        .set(cite_row)
        .reshape(devices, capacity)
    )
    asked = lax.all_to_all(wanted, "dp", split_axis=0, concat_axis=0, tiled=True)
    looked = jnp.take(item_vec, asked.reshape(-1), axis=0).reshape(
        devices, capacity, item_vec.shape[1]
    )
    answers = lax.all_to_all(looked, "dp", split_axis=0, concat_axis=0, tiled=True)
    cited = jnp.take(answers.reshape(devices * capacity, item_vec.shape[1]), target, axis=0)
    cited = lax.all_gather(cited, "tp", axis=1, tiled=True)
    values32 = cited.astype(jnp.float32)
    scale = lax.rsqrt(jnp.mean(values32 * values32, axis=1, keepdims=True) + 1e-05)
    normed = (values32 * scale * user_gain[None, :]).astype(jnp.bfloat16)
    shard_rows, user_heads, triple = user_weight.shape
    weight_flat = user_weight.reshape(shard_rows, user_heads * triple)
    projected = jnp.dot(
        normed,
        lax.all_gather(weight_flat, "dp", axis=0, tiled=True),
        preferred_element_type=jnp.float32,
    )
    live = jnp.arange(length_seq, dtype=jnp.int32) < seq_length[0]
    masked = jnp.where(live[:, None], projected, jnp.zeros_like(projected))
    return masked.astype(jnp.bfloat16).reshape(length_seq, user_heads, triple)


def solution(mesh):
    in_specs = (
        P("dp", "tp"),
        P("dp", None, "tp"),
        P("dp", None, "tp"),
        P("tp", None),
        P("dp", None),
        P("dp", None),
        P("dp"),
        P("dp"),
        P(),
        P("dp", "tp", None),
    )
    out_specs = P("dp", "tp", None)
    return jax.shard_map(
        per_device, mesh=mesh, in_specs=in_specs, out_specs=out_specs, check_vma=False
    )
```

profile of v0, /device:TPU:1, one launch (start us, length us, event | category | flops | bytes accessed | tf_op | source)
XLA Modules:
  0.0 401.7 jit_solution(5603883770292417331)
XLA Ops:
  6.5 0.8 fusion.23
  7.3 18.0 %reduce-window.6 = s32[64,8,128]{2,1,0:T(8,128)S(1)} reduce-window(s32[64,8,128]{2,1,0:T(8,128)S(1)} %fusion.23, s32[]{:T(128)} %constant.20.clone.1), window={size=1x1x128 pad=0_0x0_0x127_0}, to_apply=%region_0.0 | reduce-window | flops 8323072 | bytes 524292 | tf_op jit(solution)/shard_map/reduce-window
  25.9 0.8 fusion.22
  27.4 4.5 %scatter_custom_fusion = s32[1536]{0:T(1024)S(1)} fusion(s32[1024]{0:T(1024)S(1)} %bitcast.69, s32[1024]{0:T(1024)} %param.16, s32[]{:T(128)} %constant.20.clone.1), kind=kCustom, calls=%fused_computation.46 | custom fusion | bytes 6656 | tf_op jit(solution)/shard_map/scatter | solution.py:61
  32.5 13.1 %all-to-all-start = ((s32[64,1,24]{2,1,0:T(1,128)}), s32[64,1,24]{2,1,0:T(1,128)S(1)}, u32[]{:S(2)}, u32[]{:S(2)}) async-start(s32[64,1,24]{2,1,0:T(1,128)} %bitcast.7), calls=%async_computation | async-start | bytes 65536 | tf_op jit(solution)/shard_map/all_to_all | solution.py:64
  45.7 1.3 reshape.152
  47.0 1.7 fusion.18
  49.9 6.5 %copy.29 = bf16[4096,512]{1,0:T(8,128)(2,1)} copy(bf16[4096,512]{0,1:T(8,128)(2,1)} %bitcast.59) | data formatting | bytes 8388608 | tf_op jit(solution)/shard_map/dot_general | solution.py:45
  56.4 5.0 %convolution_bitcast_fusion = f32[4,128,1024]{2,1,0:T(8,128)} fusion(bf16[128,512,1]{1,0,2:T(8,128)(2,1)S(1)} %reshape.150, bf16[4,1024,512]{2,1,0:T(8,128)(2,1)} %bitcast.57), kind=kOutput, calls=%fused_computation.16 | convolution fusion | flops 536870912 | bytes 6422528 | tf_op jit(solution)/shard_map/dot_general | solution.py:45
  61.3 4.0 %all-to-all-start.1 = ((f32[4,128,1024]{2,1,0:T(8,128)}), f32[4,128,1024]{2,1,0:T(8,128)S(1)}, u32[]{:S(2)}, u32[]{:S(2)}) async-start(f32[4,128,1024]{2,1,0:T(8,128)} %convolution_bitcast_fusion), calls=%async_computation.1 | async-start | bytes 4194304 | tf_op jit(solution)/shard_map/all_to_all | solution.py:17
  66.0 0.8 reduce.7
  66.9 24.2 %all-to-all-done.1 = f32[4,128,1024]{2,1,0:T(8,128)S(1)} async-done(((f32[4,128,1024]{2,1,0:T(8,128)}), f32[4,128,1024]{2,1,0:T(8,128)S(1)}, u32[]{:S(2)}, u32[]{:S(2)}) %all-to-all-start.1) | async-done | bytes 2097184 | tf_op jit(solution)/shard_map/all_to_all | solution.py:17
  91.3 1.0 add_convert_fusion
  92.3 5.8 %gather_fusion = bf16[1536,1024]{1,0:T(8,128)(2,1)} fusion(bf16[128,1024]{1,0:T(8,128)(2,1)S(1)} %add_convert_fusion, s32[2048]{0:T(1024)S(1)} %pad_clamp_fusion), kind=kCustom, calls=%fused_computation | custom fusion | bytes 6297600 | tf_op jit(solution)/shard_map/jit(_take)/gather | solution.py:65
  98.1 3.3 broadcast_select_fusion
  101.3 11.7 %all-to-all-start.2 = ((bf16[64,24,1024]{2,1,0:T(8,128)(2,1)}), bf16[64,24,1024]{2,1,0:T(8,128)(2,1)}, u32[]{:S(2)}, u32[]{:S(2)}) async-start(bf16[64,24,1024]{2,1,0:T(8,128)(2,1)} %broadcast_select_fusion), calls=%async_computation.2 | async-start | bytes 6291456 | tf_op jit(solution)/shard_map/all_to_all | solution.py:68
  113.1 72.3 %all-to-all-done.2 = bf16[64,24,1024]{2,1,0:T(8,128)(2,1)} async-done(((bf16[64,24,1024]{2,1,0:T(8,128)(2,1)}), bf16[64,24,1024]{2,1,0:T(8,128)(2,1)}, u32[]{:S(2)}, u32[]{:S(2)}) %all-to-all-start.2) | async-done | bytes 3145760 | tf_op jit(solution)/shard_map/all_to_all | solution.py:68
  185.4 7.3 %gather_fusion.1 = bf16[1024,1024]{1,0:T(8,128)(2,1)S(1)} fusion(bf16[1536,1024]{1,0:T(8,128)(2,1)} %bitcast.19, s32[1024]{0:T(1024)S(1)} %broadcast_clamp_fusion), kind=kCustom, calls=%fused_computation.1 | custom fusion | bytes 4198400 | tf_op jit(solution)/shard_map/jit(_take)/gather | solution.py:69
  192.7 1.6 broadcast_select_fusion.1
  195.9 79.5 %all-gather.3.cloned.1.call-done = bf16[1024,4096]{1,0:T(8,128)(2,1)} async-done(((bf16[1024,1024]{1,0:T(8,128)(2,1)}), bf16[1024,4096]{1,0:T(8,128)(2,1)}) %all-gather.3.cloned.1.call-update) | async-done | bytes 8388624 | tf_op jit(solution)/shard_map/all_gather | solution.py:70
  275.4 5.1 %fusion.2 = f32[1024]{0:T(1024)S(1)} fusion(bf16[1024,4096]{1,0:T(8,128)(2,1)} %all-gather.3.cloned.1.call-done), kind=kLoop, calls=%fused_computation.7 | loop fusion | flops 12581888 | bytes 8392704 | tf_op jit(solution)/shard_map/reduce_sum | solution.py:72
  280.5 88.8 %all-gather.5.cloned.1.call-done = bf16[4096,1536]{1,0:T(8,128)(2,1)} async-done(((bf16[64,1536]{1,0:T(8,128)(2,1)}), bf16[4096,1536]{1,0:T(8,128)(2,1)}) %all-gather.5.cloned.1.call-update) | async-done | bytes 12582928 | tf_op jit(solution)/shard_map/all_gather | solution.py:78
  369.3 19.3 %select_convert_fusion = bf16[1024,1536]{1,0:T(8,128)(2,1)} fusion(bf16[4096,1536]{1,0:T(8,128)(2,1)} %all-gather.5.cloned.1.call-done, bf16[1024,4096]{1,0:T(8,128)(2,1)} %all-gather.3.cloned.1.call-done, f32[4096]{0:T(1024)S(1)} %copy-done.2, f32[1024]{0:T(1024)S(1)} %add_rsqrt_fusion, pred[1024]{0:T(1024)(128)(4,1)S(1)} %iota_compare_fusion.2), kind=kOutput, calls=%fused_computation.13 | convolution fusion | flops 12904824832 | bytes 24138752 | tf_op jit(solution)/shard_map/dot_general | solution.py:76
  388.6 6.2 %reshape.121 = bf16[1024,4,384]{2,1,0:T(4,128)(2,1)} reshape(bf16[1024,1536]{1,0:T(8,128)(2,1)} %select_convert_fusion) | data formatting | bytes 6291456 | tf_op jit(solution)/shard_map/reshape | solution.py:83
  (35 shorter events, 5.0 us)
Async XLA Ops:
  6.5 42.5 %copy-start = (bf16[128,4,512]{2,1,0:T(4,128)(2,1)S(1)}, bf16[128,4,512]{2,1,0:T(4,128)(2,1)}, u32[]{:S(2)}) copy-start(bf16[128,4,512]{2,1,0:T(4,128)(2,1)} %param.12) | copy-start | bytes 1572868
  32.5 28.8 %all-to-all-start = ((s32[64,1,24]{2,1,0:T(1,128)}), s32[64,1,24]{2,1,0:T(1,128)S(1)}, u32[]{:S(2)}, u32[]{:S(2)}) async-start(s32[64,1,24]{2,1,0:T(1,128)} %bitcast.7), calls=%async_computation | async-start | bytes 65536 | tf_op jit(solution)/shard_map/all_to_all | solution.py:64
  61.3 29.7 %all-to-all-start.1 = ((f32[4,128,1024]{2,1,0:T(8,128)}), f32[4,128,1024]{2,1,0:T(8,128)S(1)}, u32[]{:S(2)}, u32[]{:S(2)}) async-start(f32[4,128,1024]{2,1,0:T(8,128)} %convolution_bitcast_fusion), calls=%async_computation.1 | async-start | bytes 4194304 | tf_op jit(solution)/shard_map/all_to_all | solution.py:17
  101.3 84.0 %all-to-all-start.2 = ((bf16[64,24,1024]{2,1,0:T(8,128)(2,1)}), bf16[64,24,1024]{2,1,0:T(8,128)(2,1)}, u32[]{:S(2)}, u32[]{:S(2)}) async-start(bf16[64,24,1024]{2,1,0:T(8,128)(2,1)} %broadcast_select_fusion), calls=%async_computation.2 | async-start | bytes 6291456 | tf_op jit(solution)/shard_map/all_to_all | solution.py:68
  113.0 162.4 %all-gather.3.cloned.1.call-start = ((), (), s32[]{:S(2)}) async-start(), calls=%async_computation.3 | async-start | bytes 10485760 | tf_op jit(solution)/shard_map/all_gather | solution.py:70
  192.7 1.9 copy-start.1
  194.3 175.0 %all-gather.5.cloned.1.call-start = ((), (), s32[]{:S(2)}) async-start(), calls=%async_computation.4 | async-start | bytes 12779520 | tf_op jit(solution)/shard_map/all_gather | solution.py:78
  195.9 173.3 %copy-start.2 = (f32[4096]{0:T(1024)S(1)}, f32[4096]{0:T(1024)}, u32[]{:S(2)}) copy-start(f32[4096]{0:T(1024)} %param.18) | copy-start | bytes 49156
Sparse Core Ops, SparseCore 0:
  194.4 80.9 all-gather.2
  278.1 91.0 all-gather.4
where the time goes:
time: 403 us; the launch traced here: 402 us
  waiting for transfers between devices  265 us (66%)
  local copies, waits for them, and re-layouts  34.3 us (9%)
  other arithmetic  32.5 us (8%)
  starting transfers between devices  29.1 us (7%)
  matrix products  26.7 us (7%)
  between operations  14.3 us (4%)
    all_gather x1, waiting for transfers between devices, per_device(): lax.all_gather(weight_flat, 'dp', axis=0, tiled=True)  88.8 us
    all_gather x1, waiting for transfers between devices, per_device(): cited = lax.all_gather(cited, 'tp', axis=1, tiled=True)  79.5 us
    all_to_all x1, waiting for transfers between devices, per_device(): lax.all_to_all(looked, 'dp', split_axis=0, concat_axis=0, tiled=True)  72.3 us
    all_to_all x1, waiting for transfers between devices, sent_and_summed(): lax.all_to_all(parts, axis, split_axis=0, concat_axis=0, tiled=True)  24.2 us
    dot_general x1, matrix products, per_device(): jnp.dot(normed, lax.all_gather(weight_flat, 'dp', axis=0, tiled=True), pr...  19.3 us
    another operation x3, other arithmetic  18.2 us
    all_to_all x1, starting transfers between devices, per_device(): lax.all_to_all(wanted, 'dp', split_axis=0, concat_axis=0, tiled=True)  13.1 us
    all_to_all x1, starting transfers between devices, per_device(): lax.all_to_all(looked, 'dp', split_axis=0, concat_axis=0, tiled=True)  11.7 us
  transfers between devices with their start and end apart: 5, of which 4 were waited for; matrix products, arithmetic and copies ran while one was open for 6% of the time, Pallas kernels for 0%

commit v1 on v0

--- a/solution.py
+++ b/solution.py
@@ -67,7 +67,9 @@
     )
     answers = lax.all_to_all(looked, "dp", split_axis=0, concat_axis=0, tiled=True)
     cited = jnp.take(answers.reshape(devices * capacity, item_vec.shape[1]), target, axis=0)
-    cited = lax.all_gather(cited, "tp", axis=1, tiled=True)
+    cited = jnp.concatenate(
+        lax.all_to_all(jnp.stack([cited] * lax.axis_size("tp")), "tp", 0, 0), axis=1
+    )
     values32 = cited.astype(jnp.float32)
     scale = lax.rsqrt(jnp.mean(values32 * values32, axis=1, keepdims=True) + 1e-05)
     normed = (values32 * scale * user_gain[None, :]).astype(jnp.bfloat16)

time: 403 us -> 343 us (0.85)
  waiting for transfers between devices: 265 us -> 188 us
  other arithmetic: 32.5 us -> 40.3 us
  starting transfers between devices: 29.1 us -> 34.5 us
  local copies, waits for them, and re-layouts: 34.3 us -> 38.6 us
    all_to_all x0 -> x1, waiting for transfers between devices: none -> 91.2 us  [per_device(): lax.all_to_all(jnp.stack([cited] * lax.axis_size('tp')), 'tp', 0, 0)]
    all_gather x1, waiting for transfers between devices: 88.8 us -> 0.01 us  [per_device(): lax.all_gather(weight_flat, 'dp', axis=0, tiled=True)]
    all_gather x1 -> x0, waiting for transfers between devices: 79.5 us -> none  [per_device(): cited = lax.all_gather(cited, 'tp', axis=1, tiled=True)]
    convert_element_type x0 -> x1, other arithmetic: none -> 7.68 us  [per_device(): normed = (values32 * scale * user_gain[None, :]).astype(jnp.bfloat16)]
    all_to_all x0 -> x1, starting transfers between devices: none -> 5.81 us  [per_device(): lax.all_to_all(jnp.stack([cited] * lax.axis_size('tp')), 'tp', 0, 0)]
    another operation x2 -> x3, local copies, waits for them, and re-layouts: 0.09 us -> 4.38 us  [the longest x1 4.3 us: per_device(): jnp.stack([cited] * lax.axis_size('tp'))]
  transfers between devices with their start and end apart: 5 -> 5, of which waited for: 4 -> 3; matrix products, arithmetic and copies ran while one was open for 6% -> 22% of each run, Pallas kernels for 0% -> 0%
where the time goes in v1:
time: 343 us; the launch traced here: 341 us
  waiting for transfers between devices  188 us (55%)
  other arithmetic  40.3 us (12%)
  local copies, waits for them, and re-layouts  38.6 us (11%)
  starting transfers between devices  34.5 us (10%)
  matrix products  25.7 us (7%)
  between operations  14.3 us (4%)
    all_to_all x1, waiting for transfers between devices, per_device(): lax.all_to_all(jnp.stack([cited] * lax.axis_size('tp')), 'tp', 0, 0)  91.2 us
    all_to_all x1, waiting for transfers between devices, per_device(): lax.all_to_all(looked, 'dp', split_axis=0, concat_axis=0, tiled=True)  72.4 us
    all_to_all x1, waiting for transfers between devices, sent_and_summed(): lax.all_to_all(parts, axis, split_axis=0, concat_axis=0, tiled=True)  24.3 us
    dot_general x1, matrix products, per_device(): jnp.dot(normed, lax.all_gather(weight_flat, 'dp', axis=0, tiled=True), pr...  19.4 us
    another operation x3, other arithmetic  18.2 us
    all_to_all x1, starting transfers between devices, per_device(): lax.all_to_all(wanted, 'dp', split_axis=0, concat_axis=0, tiled=True)  13.1 us
    all_to_all x1, starting transfers between devices, per_device(): lax.all_to_all(looked, 'dp', split_axis=0, concat_axis=0, tiled=True)  11.5 us
    convert_element_type x1, other arithmetic, per_device(): normed = (values32 * scale * user_gain[None, :]).astype(jnp.bfloat16)  7.68 us
  transfers between devices with their start and end apart: 5, of which 3 were waited for; matrix products, arithmetic and copies ran while one was open for 22% of the time, Pallas kernels for 0%

profile of v1, /device:TPU:1, one launch (start us, length us, event | category | flops | bytes accessed | tf_op | source)
XLA Modules:
  0.0 341.2 jit_solution(8499331383739037250)
XLA Ops:
  6.5 1.7 copy.34
  9.0 18.0 %reduce-window.6 = s32[64,8,128]{2,1,0:T(8,128)S(1)} reduce-window(s32[64,8,128]{2,1,0:T(8,128)S(1)} %fusion.16, s32[]{:T(128)} %constant.20.clone.1), window={size=1x1x128 pad=0_0x0_0x127_0}, to_apply=%region_0.0 | reduce-window | flops 8323072 | bytes 524292 | tf_op jit(solution)/shard_map/reduce-window
  27.5 0.8 fusion.15
  29.0 4.5 %scatter_custom_fusion = s32[1536]{0:T(1024)S(1)} fusion(s32[1024]{0:T(1024)S(1)} %bitcast.78, s32[1024]{0:T(1024)} %param.16, s32[]{:T(128)} %constant.20.clone.1), kind=kCustom, calls=%fused_computation.42 | custom fusion | bytes 6656 | tf_op jit(solution)/shard_map/scatter | solution.py:61
  34.2 13.1 %all-to-all-start = ((s32[64,1,24]{2,1,0:T(1,128)}), s32[64,1,24]{2,1,0:T(1,128)S(1)}, u32[]{:S(2)}, u32[]{:S(2)}) async-start(s32[64,1,24]{2,1,0:T(1,128)} %bitcast.7), calls=%async_computation | async-start | bytes 65536 | tf_op jit(solution)/shard_map/all_to_all | solution.py:64
  47.4 6.6 %copy.32 = bf16[4096,512]{1,0:T(8,128)(2,1)} copy(bf16[4096,512]{0,1:T(8,128)(2,1)} %bitcast.68) | data formatting | bytes 8388608 | tf_op jit(solution)/shard_map/dot_general | solution.py:45
  55.9 5.0 %convolution_bitcast_fusion = f32[4,128,1024]{2,1,0:T(8,128)} fusion(bf16[128,512,1]{1,0,2:T(8,128)(2,1)S(1)} %reshape.163, bf16[4,1024,512]{2,1,0:T(8,128)(2,1)} %bitcast.66), kind=kOutput, calls=%fused_computation.12 | convolution fusion | flops 536870912 | bytes 6422528 | tf_op jit(solution)/shard_map/dot_general | solution.py:45
  60.9 4.0 %all-to-all-start.1 = ((f32[4,128,1024]{2,1,0:T(8,128)}), f32[4,128,1024]{2,1,0:T(8,128)S(1)}, u32[]{:S(2)}, u32[]{:S(2)}) async-start(f32[4,128,1024]{2,1,0:T(8,128)} %convolution_bitcast_fusion), calls=%async_computation.1 | async-start | bytes 4194304 | tf_op jit(solution)/shard_map/all_to_all | solution.py:17
  66.3 24.3 %all-to-all-done.1 = f32[4,128,1024]{2,1,0:T(8,128)S(1)} async-done(((f32[4,128,1024]{2,1,0:T(8,128)}), f32[4,128,1024]{2,1,0:T(8,128)S(1)}, u32[]{:S(2)}, u32[]{:S(2)}) %all-to-all-start.1) | async-done | bytes 2097184 | tf_op jit(solution)/shard_map/all_to_all | solution.py:17
  90.8 1.0 add_convert_fusion
  91.8 5.1 %gather_fusion = bf16[1536,1024]{1,0:T(8,128)(2,1)S(1)} fusion(bf16[128,1024]{1,0:T(8,128)(2,1)S(1)} %add_convert_fusion, s32[2048]{0:T(1024)S(1)} %pad_clamp_fusion), kind=kCustom, calls=%fused_computation | custom fusion | bytes 6297600 | tf_op jit(solution)/shard_map/jit(_take)/gather | solution.py:65
  96.9 1.9 broadcast_select_fusion
  98.8 11.5 %all-to-all-start.2 = ((bf16[64,24,1024]{2,1,0:T(8,128)(2,1)}), bf16[64,24,1024]{2,1,0:T(8,128)(2,1)S(1)}, u32[]{:S(2)}, u32[]{:S(2)}) async-start(bf16[64,24,1024]{2,1,0:T(8,128)(2,1)} %broadcast_select_fusion), calls=%async_computation.2 | async-start | bytes 6291456 | tf_op jit(solution)/shard_map/all_to_all | solution.py:68
  110.3 72.4 %all-to-all-done.2 = bf16[64,24,1024]{2,1,0:T(8,128)(2,1)S(1)} async-done(((bf16[64,24,1024]{2,1,0:T(8,128)(2,1)}), bf16[64,24,1024]{2,1,0:T(8,128)(2,1)S(1)}, u32[]{:S(2)}, u32[]{:S(2)}) %all-to-all-start.2) | async-done | bytes 3145760 | tf_op jit(solution)/shard_map/all_to_all | solution.py:68
  182.7 5.3 %gather_fusion.1 = bf16[1024,1024]{1,0:T(8,128)(2,1)} fusion(bf16[1536,1024]{1,0:T(8,128)(2,1)S(1)} %bitcast.65, s32[1024]{0:T(1024)S(1)} %broadcast_clamp_fusion), kind=kCustom, calls=%fused_computation.1 | custom fusion | bytes 4198400 | tf_op jit(solution)/shard_map/jit(_take)/gather | solution.py:69
  188.0 3.2 broadcast_select_fusion.1
  191.2 2.9 copy.25
  194.1 4.3 %stack.2 = bf16[4,1024,1024]{1,2,0:T(8,128)(2,1)} broadcast(bf16[1024,1024]{0,1:T(8,128)(2,1)S(1)} %copy.25), dimensions={1,2} | broadcast | bytes 10485760 | tf_op jit(solution)/shard_map/stack | solution.py:71
  198.4 5.8 %all-to-all-start.3 = ((bf16[4,1024,1024]{1,2,0:T(8,128)(2,1)}), bf16[4,1024,1024]{1,2,0:T(8,128)(2,1)}, u32[]{:S(2)}, u32[]{:S(2)}) async-start(bf16[4,1024,1024]{1,2,0:T(8,128)(2,1)} %stack.2), calls=%async_computation.3 | async-start | bytes 16777216 | tf_op jit(solution)/shard_map/all_to_all | solution.py:71
  204.9 91.2 %all-to-all-done.3 = bf16[4,1024,1024]{1,2,0:T(8,128)(2,1)} async-done(((bf16[4,1024,1024]{1,2,0:T(8,128)(2,1)}), bf16[4,1024,1024]{1,2,0:T(8,128)(2,1)}, u32[]{:S(2)}, u32[]{:S(2)}) %all-to-all-start.3) | async-done | bytes 8388640 | tf_op jit(solution)/shard_map/all_to_all | solution.py:71
  296.0 5.1 %multiply_reduce_fusion = f32[1024]{0:T(1024)S(1)} fusion(bf16[4,1024,1024]{1,2,0:T(8,128)(2,1)} %all-to-all-done.3), kind=kLoop, calls=%fused_computation.8 | loop fusion | flops 12581888 | bytes 8392704 | tf_op jit(solution)/shard_map/reduce_sum | solution.py:74
  301.1 7.7 %fusion.3 = bf16[1024,4096]{0,1:T(8,128)(2,1)} fusion(f32[4096]{0:T(1024)S(1)} %copy-done.3, f32[1024]{0:T(1024)S(1)} %add_rsqrt_fusion, bf16[4,1024,1024]{1,2,0:T(8,128)(2,1)} %all-to-all-done.3), kind=kLoop, calls=%fused_computation.7 | loop fusion | flops 16777216 | bytes 16797696 | tf_op jit(solution)/shard_map/convert_element_type | solution.py:75
  308.8 19.4 %select_convert_fusion = bf16[1024,1536]{1,0:T(8,128)(2,1)} fusion(bf16[1024,4096]{0,1:T(8,128)(2,1)} %fusion.3, bf16[4096,1536]{1,0:T(8,128)(2,1)} %all-gather.2.cloned.1.call-done, pred[1024]{0:T(1024)(128)(4,1)S(1)} %iota_compare_fusion.2), kind=kOutput, calls=%fused_computation.9 | convolution fusion | flops 12888047616 | bytes 24118272 | tf_op jit(solution)/shard_map/dot_general | solution.py:78
  328.2 6.2 %reshape.133 = bf16[1024,4,384]{2,1,0:T(4,128)(2,1)} reshape(bf16[1024,1536]{1,0:T(8,128)(2,1)} %select_convert_fusion) | data formatting | bytes 6291456 | tf_op jit(solution)/shard_map/reshape | solution.py:85
  (41 shorter events, 6.1 us)
Async XLA Ops:
  6.5 48.5 %copy-start = (bf16[128,4,512]{2,1,0:T(4,128)(2,1)S(1)}, bf16[128,4,512]{2,1,0:T(4,128)(2,1)}, u32[]{:S(2)}) copy-start(bf16[128,4,512]{2,1,0:T(4,128)(2,1)} %param.12) | copy-start | bytes 1572868
  6.5 302.3 %all-gather.2.cloned.1.call-start = ((), (), s32[]{:S(2)}) async-start(), calls=%async_computation.4 | async-start | bytes 12779520 | tf_op jit(solution)/shard_map/all_gather | solution.py:80
  34.2 26.7 %all-to-all-start = ((s32[64,1,24]{2,1,0:T(1,128)}), s32[64,1,24]{2,1,0:T(1,128)S(1)}, u32[]{:S(2)}, u32[]{:S(2)}) async-start(s32[64,1,24]{2,1,0:T(1,128)} %bitcast.7), calls=%async_computation | async-start | bytes 65536 | tf_op jit(solution)/shard_map/all_to_all | solution.py:64
  47.3 6.6 %copy-start.2 = (bf16[128,512]{1,0:T(8,128)(2,1)S(1)}, bf16[128,512]{1,0:T(8,128)(2,1)}, u32[]{:S(2)}) copy-start(bf16[128,512]{1,0:T(8,128)(2,1)} %param.10) | copy-start | bytes 393220
  47.3 6.6 %copy-start.4 = (bf16[128,4,512]{2,1,0:T(4,128)(2,1)S(1)}, bf16[128,4,512]{2,1,0:T(4,128)(2,1)}, u32[]{:S(2)}) copy-start(bf16[128,4,512]{2,1,0:T(4,128)(2,1)} %param.11) | copy-start | bytes 1572868
  60.9 29.7 %all-to-all-start.1 = ((f32[4,128,1024]{2,1,0:T(8,128)}), f32[4,128,1024]{2,1,0:T(8,128)S(1)}, u32[]{:S(2)}, u32[]{:S(2)}) async-start(f32[4,128,1024]{2,1,0:T(8,128)} %convolution_bitcast_fusion), calls=%async_computation.1 | async-start | bytes 4194304 | tf_op jit(solution)/shard_map/all_to_all | solution.py:17
  98.8 83.9 %all-to-all-start.2 = ((bf16[64,24,1024]{2,1,0:T(8,128)(2,1)}), bf16[64,24,1024]{2,1,0:T(8,128)(2,1)S(1)}, u32[]{:S(2)}, u32[]{:S(2)}) async-start(bf16[64,24,1024]{2,1,0:T(8,128)(2,1)} %broadcast_select_fusion), calls=%async_computation.2 | async-start | bytes 6291456 | tf_op jit(solution)/shard_map/all_to_all | solution.py:68
  198.4 97.7 %all-to-all-start.3 = ((bf16[4,1024,1024]{1,2,0:T(8,128)(2,1)}), bf16[4,1024,1024]{1,2,0:T(8,128)(2,1)}, u32[]{:S(2)}, u32[]{:S(2)}) async-start(bf16[4,1024,1024]{1,2,0:T(8,128)(2,1)} %stack.2), calls=%async_computation.3 | async-start | bytes 16777216 | tf_op jit(solution)/shard_map/all_to_all | solution.py:71
  204.8 96.3 %copy-start.3 = (f32[4096]{0:T(1024)S(1)}, f32[4096]{0:T(1024)}, u32[]{:S(2)}) copy-start(f32[4096]{0:T(1024)} %param.18) | copy-start | bytes 49156
  308.8 25.6 %copy-start.1 = (bf16[128,4,512]{2,1,0:T(4,128)(2,1)S(1)}, bf16[128,4,512]{2,1,0:T(4,128)(2,1)}, u32[]{:S(2)}) copy-start(bf16[128,4,512]{2,1,0:T(4,128)(2,1)} %param.12) | copy-start | bytes 1572868
Sparse Core Ops, SparseCore 0:
  10.1 93.7 all-gather.1
